TPU v7x, 256 devices: a whole 4x4x8 slice. The times are simulated.
256 devices in a mesh: row: 16 (over y, x), col: 8 (over z), rep: 2 (over core).
Axes of the slice: x: 4, y: 4, z: 8, core: 2. Of those that a mesh axis runs over, the one named last changes fastest.
Arguments:
- patches: bfloat16 [2, 512, 6144], P('rep', 'col', 'row'), may hold values from -6 to 6
- cotangent: bfloat16 [2, 512, 6144], P('rep', 'col', 'row'), may hold values from -6 to 6
- w_in: bfloat16 [6144, 24576], P('row', 'col'), may hold values from -0.078125 to 0.078125
- w_out: bfloat16 [24576, 6144], P('col', 'row'), may hold values from -0.0390625 to 0.0390625
- moment_in: bfloat16 [2, 6144, 24576], P('rep', 'row', 'col'), may hold values from -2 to 2
- moment_out: bfloat16 [2, 24576, 6144], P('rep', 'col', 'row'), may hold values from -2 to 2
Outputs:
- mixed: bfloat16 [2, 512, 6144], P('rep', 'col', 'row')
- tally_in: bfloat16 [6144, 24576], P('row', 'col')
- tally_out: bfloat16 [24576, 6144], P('col', 'row')
All inputs are finite; a program needn't handle non-finite values.
Results may differ from a plain program's by a relative error of at most 0.0055.
Values may be sent and summed in bfloat16 or wider, within the bound.
A program may use at most 128 MiB of HBM per device.

v0:
```python
import math
import jax
import jax.numpy as jnp
from jax import lax
from jax.sharding import PartitionSpec as P

momentum_decay = 0.9
vote_scale = 0.3


def joined_along(blocks, dim):
    blocks = jnp.moveaxis(blocks, 0, dim)
    lengths = blocks.shape
    return blocks.reshape(*lengths[:dim], lengths[dim] * lengths[dim + 1], *lengths[dim + 2 :])


def sent_to_all(value, axis):
    copies = jnp.broadcast_to(value, (lax.axis_size(axis), *value.shape))
    return lax.all_to_all(copies, axis, split_axis=0, concat_axis=0, tiled=True)


def gather_directly(value, axis, dim):
    return joined_along(sent_to_all(value, axis), dim)


def cut_along(value, dim, peers):
    before, after = (value.shape[:dim], value.shape[dim + 1 :])
    return jnp.moveaxis(value.reshape(*before, peers, -1, *after), dim, 0)


def sum_at_owner(value, axis, dim):
    blocks = cut_along(value, dim, lax.axis_size(axis))
    arrived = lax.all_to_all(blocks, axis, split_axis=0, concat_axis=0, tiled=True)
    return arrived.sum(axis=0)


def gelu_value(pre):
    return 0.5 * pre * (1.0 + lax.erf(pre * (1.0 / math.sqrt(2.0))))


def gelu_slope(pre):
    return 0.5 * (1.0 + lax.erf(pre * (1.0 / math.sqrt(2.0)))) + pre * jnp.exp(-0.5 * pre * pre) * (
        1.0 / math.sqrt(2.0 * math.pi)
    )


def shards(patches, cotangent, w_in, w_out, moment_in, moment_out):
    inputs = gather_directly(patches[0], "col", 0)
    total_rows = inputs.shape[0]
    norm_factor = 1.0 / math.sqrt(total_rows)
    pre_whole = lax.psum(jnp.dot(inputs, w_in, preferred_element_type=jnp.float32), "row")
    hidden = gelu_value(pre_whole).astype(jnp.bfloat16)
    block = hidden
    mixed = sum_at_owner(
        jnp.dot(block, w_out, preferred_element_type=jnp.float32), "col", 0
    ).astype(jnp.bfloat16)
    grads = lax.all_gather(cotangent[0], "col", axis=0, tiled=True)
    block = grads
    back_whole = lax.psum(
        lax.dot_general(
            block, w_out, (((1,), (1,)), ((), ())), preferred_element_type=jnp.float32
        ).astype(jnp.bfloat16),
        "row",
    ).astype(jnp.float32)
    slope = (back_whole * gelu_slope(pre_whole)).astype(jnp.bfloat16)
    grad_first = (
        lax.dot_general(inputs, slope, (((0,), (0,)), ((), ())), preferred_element_type=jnp.float32)
        * norm_factor
    )
    grad_second = (
        lax.dot_general(hidden, grads, (((0,), (0,)), ((), ())), preferred_element_type=jnp.float32)
        * norm_factor
    )
    moved_first = (
        momentum_decay * moment_in[0].astype(jnp.float32) + (1.0 - momentum_decay) * grad_first
    )
    moved_second = (
        momentum_decay * moment_out[0].astype(jnp.float32) + (1.0 - momentum_decay) * grad_second
    )
    vote_first = jnp.tanh(moved_first / vote_scale).astype(jnp.bfloat16)
    vote_second = jnp.tanh(moved_second / vote_scale).astype(jnp.bfloat16)
    tally_first, tally_second = (
        lax.psum(vote_first, "rep").astype(jnp.float32),
        lax.psum(vote_second, "rep").astype(jnp.float32),
    )
    return (mixed[None], tally_first.astype(jnp.bfloat16), tally_second.astype(jnp.bfloat16))


def solution(mesh):
    in_specs = (
        P("rep", "col", "row"),
        P("rep", "col", "row"),
        P("row", "col"),
        P("col", "row"),
        P("rep", "row", "col"),
        P("rep", "col", "row"),
    )
    out_specs = (P("rep", "col", "row"), P("row", "col"), P("col", "row"))
    return jax.shard_map(shards, mesh=mesh, in_specs=in_specs, out_specs=out_specs, check_vma=False)
```

profile of v0, /device:TPU:1, one launch (start us, length us, event | category | flops | bytes accessed | tf_op | source)
XLA Modules:
  0.0 338.2 jit_solution(2649844550422343762)
XLA Ops:
  7.2 0.0 copy-start
  7.2 0.0 all-reduce.5.cloned.1.call-start
  7.2 1.0 broadcast_in_dim.4
  8.2 22.4 %all_to_all.10 = bf16[8,64,384]{2,1,0:T(8,128)(2,1)S(1)} all-to-all(bf16[8,64,384]{2,1,0:T(8,128)(2,1)S(1)} %broadcast_in_dim.4), channel_id=1, replica_groups=mesh['row'=16,'col'=8,'rep'=2] {'col'}, dimensions={0} | all-to-all | bytes 786432 | tf_op jit(solution)/shard_map/all_to_all | solution.py:19
  30.6 6.1 %fusion.20 = f32[512,3072]{1,0:T(8,128)} fusion(bf16[512,384]{1,0:T(8,128)(2,1)S(1)} %bitcast.36, bf16[384,3072]{1,0:T(8,128)(2,1)} %param.8), kind=kOutput, calls=%fused_computation.26 | convolution fusion | flops 1207959552 | bytes 9043968 | tf_op jit(solution)/shard_map/dot_general | solution.py:51
  36.7 0.0 copy-start.2
  36.7 0.0 all-reduce.5.cloned.1.call-update
  36.7 0.0 all-reduce.7.cloned.1.call-start
  36.8 0.7 copy-done.2
  37.5 20.5 %all-gather = bf16[1,512,384]{2,1,0:T(8,128)(2,1)S(1)} all-gather(bf16[1,64,384]{2,1,0:T(8,128)(2,1)S(1)} %copy-done.2), channel_id=2, replica_groups=mesh['row'=16,'col'=8,'rep'=2] {'col'}, dimensions={1}, use_global_device_ids=true | all-gather | bytes 442368 | tf_op jit(solution)/shard_map/all_gather | solution.py:57
  58.0 0.0 copy-done
  58.0 3.5 %convolution_convert_fusion = bf16[512,3072]{1,0:T(8,128)(2,1)} fusion(bf16[3072,384]{1,0:T(8,128)(2,1)S(1)} %copy-done, bf16[1,512,384]{2,1,0:T(8,128)(2,1)S(1)} %all-gather), kind=kOutput, calls=%fused_computation.17 | convolution fusion | flops 1209532416 | bytes 5898240 | tf_op jit(solution)/shard_map/dot_general | solution.py:60
  61.4 0.0 all-reduce.7.cloned.1.call-update
  61.5 0.0 all-reduce.9.cloned.1.call-start
  61.5 4.3 %copy.9 = bf16[1,384,3072]{1,2,0:T(8,128)(2,1)} copy(bf16[1,384,3072]{2,1,0:T(8,128)(2,1)} %param.10) | data formatting | bytes 4718592 | tf_op args[4]
  65.8 101.0 %all-reduce.5.cloned.1.call-done = f32[512,3072]{1,0:T(8,128)} async-done(((f32[512,3072]{1,0:T(8,128)}), f32[512,3072]{1,0:T(8,128)}) %all-reduce.5.cloned.1.call-update) | async-done | bytes 6291472 | tf_op jit(solution)/shard_map/psum | solution.py:51
  166.8 0.0 copy-start.3
  166.8 3.6 %multiply_convert_fusion = bf16[512,3072]{1,0:T(8,128)(2,1)S(1)} fusion(f32[512,3072]{1,0:T(8,128)} %all-reduce.5.cloned.1.call-done), kind=kLoop, calls=%fused_computation.7 | loop fusion | flops 7864320 | bytes 9437184 | tf_op jit(solution)/shard_map/convert_element_type | solution.py:52
  170.4 0.0 copy-start.1
  170.4 1.7 copy-done.1
  172.1 0.0 copy-done.3
  172.1 4.0 %fusion.8 = bf16[3072,384]{1,0:T(8,128)(2,1)} fusion(bf16[1,3072,384]{2,1,0:T(8,128)(2,1)S(1)} %copy-done.3, bf16[512,3072]{1,0:T(8,128)(2,1)S(1)} %multiply_convert_fusion, bf16[1,512,384]{2,1,0:T(8,128)(2,1)S(1)} %all-gather), kind=kOutput, calls=%fused_computation.12 | convolution fusion | flops 1215037440 | bytes 8257536 | tf_op jit(solution)/shard_map/dot_general | solution.py:71
  176.1 99.6 %all-reduce.7.cloned.1.call-done = bf16[512,3072]{1,0:T(8,128)(2,1)} async-done(((bf16[512,3072]{1,0:T(8,128)(2,1)}), bf16[512,3072]{1,0:T(8,128)(2,1)}) %all-reduce.7.cloned.1.call-update) | async-done | bytes 3145744 | tf_op jit(solution)/shard_map/psum | solution.py:59
  275.7 8.4 %fusion.11 = bf16[384,3072]{0,1:T(8,128)(2,1)} fusion(bf16[1,384,3072]{1,2,0:T(8,128)(2,1)} %copy.9, bf16[512,384]{1,0:T(8,128)(2,1)S(1)} %bitcast.37, f32[512,3072]{1,0:T(8,128)} %all-reduce.5.cloned.1.call-done, bf16[512,3072]{1,0:T(8,128)(2,1)} %all-reduce.7.cloned.1.call-done), kind=kOutput, calls=%fused_computation.16 | convolution fusion | flops 1232338944 | bytes 14548992 | tf_op jit(solution)/shard_map/dot_general | solution.py:67
  284.1 0.0 all-reduce.9.cloned.1.call-update
  284.1 3.7 %fusion.21 = f32[512,384]{1,0:T(8,128)S(1)} fusion(bf16[512,3072]{1,0:T(8,128)(2,1)} %copy-done.1, bf16[3072,384]{1,0:T(8,128)(2,1)S(1)} %copy-done), kind=kOutput, calls=%fused_computation.27 | convolution fusion | flops 1207959552 | bytes 6291456 | tf_op jit(solution)/shard_map/dot_general | solution.py:55
  287.8 27.9 %all_to_all.11 = f32[8,64,384]{2,1,0:T(8,128)S(1)} all-to-all(f32[8,64,384]{2,1,0:T(8,128)S(1)} %bitcast.38), channel_id=1, replica_groups=mesh['row'=16,'col'=8,'rep'=2] {'col'}, dimensions={0} | all-to-all | bytes 1572864 | tf_op jit(solution)/shard_map/all_to_all | solution.py:33
  315.7 0.7 reduce_sum.9
  316.4 7.7 %all-reduce.9.cloned.1.call-done = (bf16[384,3072]{0,1:T(8,128)(2,1)}, bf16[3072,384]{1,0:T(8,128)(2,1)}) async-done(((bf16[384,3072]{0,1:T(8,128)(2,1)}, bf16[3072,384]{1,0:T(8,128)(2,1)}), (bf16[384,3072]{0,1:T(8,128)(2,1)}, bf16[3072,384]{1,0:T(8,128)(2,1)})) %all-reduce.9.cloned.1.call-update) | async-done | bytes 4718608 | tf_op jit(solution)/shard_map/psum | solution.py:83
  324.1 4.3 %copy.10 = bf16[384,3072]{1,0:T(8,128)(2,1)} copy(bf16[384,3072]{0,1:T(8,128)(2,1)} %get-tuple-element.6) | data formatting | bytes 4718592
  328.4 3.3 copy.15
Async XLA Ops:
  7.2 50.8 %copy-start = (bf16[3072,384]{1,0:T(8,128)(2,1)S(1)}, bf16[3072,384]{1,0:T(8,128)(2,1)}, u32[]{:S(2)}) copy-start(bf16[3072,384]{1,0:T(8,128)(2,1)} %param.9) | copy-start | bytes 7077892
  7.2 159.7 %all-reduce.5.cloned.1.call-start = ((), (), s32[]{:S(2)}) async-start(), calls=%async_computation.2 | async-start | bytes 12582912 | tf_op jit(solution)/shard_map/psum | solution.py:51
  36.7 0.8 copy-start.2
  36.7 239.0 %all-reduce.7.cloned.1.call-start = ((), (), s32[]{:S(2)}) async-start(), calls=%async_computation.3 | async-start | bytes 6291456 | tf_op jit(solution)/shard_map/psum | solution.py:59
  61.5 262.7 %all-reduce.9.cloned.1.call-start = ((), (), s32[]{:S(2)}) async-start(), calls=%async_computation.4 | async-start | bytes 9437184 | tf_op jit(solution)/shard_map/psum | solution.py:83
  166.8 5.3 %copy-start.3 = (bf16[1,3072,384]{2,1,0:T(8,128)(2,1)S(1)}, bf16[1,3072,384]{2,1,0:T(8,128)(2,1)}, u32[]{:S(2)}) copy-start(bf16[1,3072,384]{2,1,0:T(8,128)(2,1)} %param.11) | copy-start | bytes 7077892
  170.4 1.7 copy-start.1
Sparse Core Ops, SparseCore 0:
  36.9 129.9 all-reduce.4
  170.2 105.4 all-reduce.6
  284.2 39.8 all-reduce.8
where the time goes:
time: 339 us; the launch traced here: 338 us
  waiting for transfers between devices  208 us (61%)
  blocking collectives  70.8 us (21%)
  matrix products  25.6 us (8%)
  local copies, waits for them, and re-layouts  15.3 us (5%)
  between operations  13.8 us (4%)
  other arithmetic  4.23 us (1%)
    psum x1, waiting for transfers between devices, shards(): lax.psum(jnp.dot(inputs, w_in, preferred_element_type=jnp.float32), 'row')  101 us
    psum x1, waiting for transfers between devices, shards(): lax.psum(lax.dot_general(block, w_out, (((1,), (1,)), ((), ())), preferre...  99.6 us
    all_to_all x1, blocking collectives, sum_at_owner(): lax.all_to_all(blocks, axis, split_axis=0, concat_axis=0, tiled=True)  27.9 us
    all_to_all x1, blocking collectives, sent_to_all(): return lax.all_to_all(copies, axis, split_axis=0, concat_axis=0, tiled=True)  22.4 us
    all_gather x1, blocking collectives, shards(): grads = lax.all_gather(cotangent[0], 'col', axis=0, tiled=True)  20.5 us
    unnamed x11, local copies, waits for them, and re-layouts  14.3 us
    dot_general x1, matrix products, shards(): lax.dot_general(inputs, slope, (((0,), (0,)), ((), ())), preferred_elemen...  8.39 us
    psum x1, waiting for transfers between devices, shards(): lax.psum(vote_first, 'rep').astype(jnp.float32)  7.74 us
  transfers between devices with their start and end apart: 3, of which 3 were waited for; matrix products, arithmetic and copies ran while one was open for 6% of the time, Pallas kernels for 0%

commit v1 on v0

--- a/solution.py
+++ b/solution.py
@@ -56,11 +56,14 @@
     ).astype(jnp.bfloat16)
     grads = lax.all_gather(cotangent[0], "col", axis=0, tiled=True)
     block = grads
-    back_whole = lax.psum(
-        lax.dot_general(
-            block, w_out, (((1,), (1,)), ((), ())), preferred_element_type=jnp.float32
-        ).astype(jnp.bfloat16),
-        "row",
+    back_whole = jnp.sum(
+        lax.all_gather(
+            lax.dot_general(
+                block, w_out, (((1,), (1,)), ((), ())), preferred_element_type=jnp.float32
+            ).astype(jnp.bfloat16),
+            "row",
+        ),
+        axis=0,
     ).astype(jnp.float32)
     slope = (back_whole * gelu_slope(pre_whole)).astype(jnp.bfloat16)
     grad_first = (

time: 339 us -> 539 us (1.59)
  waiting for transfers between devices: 208 us -> 390 us
  other arithmetic: 4.23 us -> 22.8 us
    all_gather x0 -> x1, waiting for transfers between devices: none -> 281 us  [shards(): lax.all_gather(lax.dot_general(block, w_out, (((1,), (1,)), ((), ())), pr...]
    psum x1 -> x0, waiting for transfers between devices: 99.6 us -> none  [shards(): lax.psum(lax.dot_general(block, w_out, (((1,), (1,)), ((), ())), preferre...]
    reduce_sum x0 -> x1, other arithmetic: none -> 18.6 us  [shards(): jnp.sum(lax.all_gather(lax.dot_general(block, w_out, (((1,), (1,)), ((),...]
  transfers between devices with their start and end apart: 3 -> 3, of which waited for: 3 -> 3; matrix products, arithmetic and copies ran while one was open for 6% -> 4% of each run, Pallas kernels for 0% -> 0%
where the time goes in v1:
time: 539 us; the launch traced here: 538 us
  waiting for transfers between devices  390 us (72%)
  blocking collectives  70.9 us (13%)
  matrix products  25.6 us (5%)
  other arithmetic  22.8 us (4%)
  local copies, waits for them, and re-layouts  15.3 us (3%)
  between operations  13.8 us (3%)
    all_gather x1, waiting for transfers between devices, shards(): lax.all_gather(lax.dot_general(block, w_out, (((1,), (1,)), ((), ())), pr...  281 us
    psum x1, waiting for transfers between devices, shards(): lax.psum(jnp.dot(inputs, w_in, preferred_element_type=jnp.float32), 'row')  101 us
    all_to_all x1, blocking collectives, sum_at_owner(): lax.all_to_all(blocks, axis, split_axis=0, concat_axis=0, tiled=True)  28 us
    all_to_all x1, blocking collectives, sent_to_all(): return lax.all_to_all(copies, axis, split_axis=0, concat_axis=0, tiled=True)  22.4 us
    all_gather x1, blocking collectives, shards(): grads = lax.all_gather(cotangent[0], 'col', axis=0, tiled=True)  20.5 us
    reduce_sum x1, other arithmetic, shards(): jnp.sum(lax.all_gather(lax.dot_general(block, w_out, (((1,), (1,)), ((),...  18.6 us
    unnamed x11, local copies, waits for them, and re-layouts  14.3 us
  transfers between devices with their start and end apart: 3, of which 3 were waited for; matrix products, arithmetic and copies ran while one was open for 4% of the time, Pallas kernels for 0%

profile of v1, /device:TPU:1, one launch (start us, length us, event | category | flops | bytes accessed | tf_op | source)
XLA Modules:
  0.0 538.5 jit_solution(16435453833850260729)
XLA Ops:
  7.2 0.0 copy-start
  7.2 0.0 all-reduce.4.cloned.1.call-start
  7.2 1.0 broadcast_in_dim.4
  8.2 22.4 %all_to_all.10 = bf16[8,64,384]{2,1,0:T(8,128)(2,1)S(1)} all-to-all(bf16[8,64,384]{2,1,0:T(8,128)(2,1)S(1)} %broadcast_in_dim.4), channel_id=1, replica_groups=mesh['row'=16,'col'=8,'rep'=2] {'col'}, dimensions={0} | all-to-all | bytes 786432 | tf_op jit(solution)/shard_map/all_to_all | solution.py:19
  30.6 6.1 %fusion.20 = f32[512,3072]{1,0:T(8,128)} fusion(bf16[512,384]{1,0:T(8,128)(2,1)S(1)} %bitcast.38, bf16[384,3072]{1,0:T(8,128)(2,1)} %param.8), kind=kOutput, calls=%fused_computation.26 | convolution fusion | flops 1207959552 | bytes 9043968 | tf_op jit(solution)/shard_map/dot_general | solution.py:51
  36.7 0.0 copy-start.2
  36.7 0.0 all-reduce.4.cloned.1.call-update
  36.7 0.0 all-gather.4.cloned.1.call-start
  36.7 0.7 copy-done.2
  37.5 20.5 %all-gather = bf16[1,512,384]{2,1,0:T(8,128)(2,1)S(1)} all-gather(bf16[1,64,384]{2,1,0:T(8,128)(2,1)S(1)} %copy-done.2), channel_id=2, replica_groups=mesh['row'=16,'col'=8,'rep'=2] {'col'}, dimensions={1}, use_global_device_ids=true | all-gather | bytes 442368 | tf_op jit(solution)/shard_map/all_gather | solution.py:57
  57.9 0.0 copy-done
  57.9 3.5 convolution_convert_fusion
  61.4 0.0 all-gather.4.cloned.1.call-update
  61.4 0.0 all-reduce.6.cloned.1.call-start
  61.5 4.3 copy.9
  65.8 101.0 %all-reduce.4.cloned.1.call-done = f32[512,3072]{1,0:T(8,128)} async-done(((f32[512,3072]{1,0:T(8,128)}), f32[512,3072]{1,0:T(8,128)}) %all-reduce.4.cloned.1.call-update) | async-done | bytes 6291472 | tf_op jit(solution)/shard_map/psum | solution.py:51
  166.8 0.0 copy-start.3
  166.8 3.6 multiply_convert_fusion
  170.4 0.0 copy-start.1
  170.4 1.7 copy-done.1
  172.0 0.0 copy-done.3
  172.0 4.0 fusion.8
  176.0 280.8 %all-gather.4.cloned.1.call-done = bf16[8192,3072]{1,0:T(8,128)(2,1)} async-done(((bf16[512,3072]{1,0:T(8,128)(2,1)}), bf16[8192,3072]{1,0:T(8,128)(2,1)}) %all-gather.4.cloned.1.call-update) | async-done | bytes 50331664 | tf_op jit(solution)/shard_map/all_gather | solution.py:60
  456.8 18.6 %reduce_sum.22 = bf16[512,3072]{1,0:T(8,128)(2,1)} reduce(bf16[16,512,3072]{2,1,0:T(8,128)(2,1)} %bitcast.37, bf16[]{:T(256)} %constant.6.clone.1), dimensions={0}, to_apply=%region_2.0 | reduce | flops 23592960 | bytes 53477376 | tf_op jit(solution)/shard_map/reduce_sum | solution.py:59
  475.4 8.4 %fusion.11 = bf16[384,3072]{0,1:T(8,128)(2,1)} fusion(bf16[1,384,3072]{1,2,0:T(8,128)(2,1)} %copy.9, bf16[512,384]{1,0:T(8,128)(2,1)S(1)} %bitcast.39, f32[512,3072]{1,0:T(8,128)} %all-reduce.4.cloned.1.call-done, bf16[512,3072]{1,0:T(8,128)(2,1)} %reduce_sum.22), kind=kOutput, calls=%fused_computation.16 | convolution fusion | flops 1232338944 | bytes 14548992 | tf_op jit(solution)/shard_map/dot_general | solution.py:70
  483.8 0.0 all-reduce.6.cloned.1.call-update
  483.8 3.7 fusion.21
  487.5 28.0 %all_to_all.11 = f32[8,64,384]{2,1,0:T(8,128)S(1)} all-to-all(f32[8,64,384]{2,1,0:T(8,128)S(1)} %bitcast.40), channel_id=1, replica_groups=mesh['row'=16,'col'=8,'rep'=2] {'col'}, dimensions={0} | all-to-all | bytes 1572864 | tf_op jit(solution)/shard_map/all_to_all | solution.py:33
  515.6 0.7 reduce_sum.21
  516.2 8.1 %all-reduce.6.cloned.1.call-done = (bf16[384,3072]{0,1:T(8,128)(2,1)}, bf16[3072,384]{1,0:T(8,128)(2,1)}) async-done(((bf16[384,3072]{0,1:T(8,128)(2,1)}, bf16[3072,384]{1,0:T(8,128)(2,1)}), (bf16[384,3072]{0,1:T(8,128)(2,1)}, bf16[3072,384]{1,0:T(8,128)(2,1)})) %all-reduce.6.cloned.1.call-update) | async-done | bytes 4718608 | tf_op jit(solution)/shard_map/psum | solution.py:86
  524.4 4.3 copy.10
  528.6 3.3 copy.14
Async XLA Ops:
  7.2 50.8 %copy-start = (bf16[3072,384]{1,0:T(8,128)(2,1)S(1)}, bf16[3072,384]{1,0:T(8,128)(2,1)}, u32[]{:S(2)}) copy-start(bf16[3072,384]{1,0:T(8,128)(2,1)} %param.9) | copy-start | bytes 7077892
  7.2 159.6 %all-reduce.4.cloned.1.call-start = ((), (), s32[]{:S(2)}) async-start(), calls=%async_computation.2 | async-start | bytes 12582912 | tf_op jit(solution)/shard_map/psum | solution.py:51
  36.7 0.8 copy-start.2
  36.7 420.2 %all-gather.4.cloned.1.call-start = ((), (), s32[]{:S(2)}) async-start(), calls=%async_computation.3 | async-start | bytes 53477376 | tf_op jit(solution)/shard_map/all_gather | solution.py:60
  61.4 462.9 %all-reduce.6.cloned.1.call-start = ((), (), s32[]{:S(2)}) async-start(), calls=%async_computation.4 | async-start | bytes 9437184 | tf_op jit(solution)/shard_map/psum | solution.py:86
  166.8 5.3 copy-start.3
  170.4 1.7 copy-start.1
Sparse Core Ops, SparseCore 0:
  36.8 129.9 all-reduce.3
  169.2 287.5 all-gather.3
  484.0 40.3 all-reduce.5
